TPU v7x, 32 devices: a whole 2x2x4 slice. The times are simulated.
32 devices in a mesh: dp: 8 (over y, x, core), mp: 4 (over z).
Axes of the slice: x: 2, y: 2, z: 4, core: 2. Of those that a mesh axis runs over, the one named last changes fastest.
Arguments:
- patches: bfloat16 [24576, 3072], P(('dp', 'mp')), may hold values from -6 to 6
- wavelengths: int32 [12], replicated, may hold values from 400 to 2499
- counts: int32 [384], P('dp'), may hold values from 1 to 64, 18432 in all
- positions: int32 [384, 64], P(('dp', 'mp')), may hold values from 0 to 195, as said below
- relation: bfloat16 [128, 384], replicated, may hold values from -1 to 1
- blending: bfloat16 [128, 128], replicated, may hold values from -0.5 to 0.5
- widening: bfloat16 [128, 2048], replicated, may hold values from -0.5 to 0.5
- narrowing: bfloat16 [2048, 128], replicated, may hold values from -0.125 to 0.125
- generator: bfloat16 [256, 128, 768], P(('dp', 'mp')), may hold values from -0.009765625 to 0.009765625
- shifting: bfloat16 [128, 768], replicated, may hold values from -0.5 to 0.5
- scaling: bfloat16 [768], replicated, may hold values from 0.25 to 1.75
- centring: bfloat16 [768], replicated, may hold values from -1.5 to 1.5
- attending: bfloat16 [768, 3, 768], P(None, None, 'mp'), may hold values from -0.21875 to 0.21875
- offsets: bfloat16 [2, 768], P(None, 'mp'), may hold values from -1.5 to 1.5
- merging: bfloat16 [768, 768], P('mp'), may hold values from -0.875 to 0.875
- lifting: bfloat16 [768], replicated, may hold values from -1.5 to 1.5
- rescaling: bfloat16 [768], replicated, may hold values from 0.25 to 1.75
- recentring: bfloat16 [768], replicated, may hold values from -1.5 to 1.5
- expanding: bfloat16 [768, 3072], P(None, 'mp'), may hold values from -0.21875 to 0.21875
- priming: bfloat16 [3072], P('mp'), may hold values from -1.5 to 1.5
- shrinking: bfloat16 [3072, 768], P('mp'), may hold values from -0.109375 to 0.109375
- settling: bfloat16 [768], replicated, may hold values from -1.5 to 1.5
- cotangent: bfloat16 [24576, 768], P(('dp', 'mp')), may hold values from -6 to 6
Outputs:
- layer_out: bfloat16 [24576, 768], P(('dp', 'mp'))
- patches_grad: float32 [24576, 3072], P(('dp', 'mp'))
- relation_grad: float32 [128, 384], replicated
- blending_grad: float32 [128, 128], replicated
- widening_grad: float32 [128, 2048], replicated
- narrowing_grad: float32 [2048, 128], replicated
- generator_grad: float32 [256, 128, 768], P(('dp', 'mp'))
- shifting_grad: float32 [128, 768], replicated
- scaling_grad: float32 [768], replicated
- centring_grad: float32 [768], replicated
- attending_grad: float32 [768, 3, 768], P(None, None, 'mp')
- offsets_grad: float32 [2, 768], P(None, 'mp')
- merging_grad: float32 [768, 768], P('mp')
- lifting_grad: float32 [768], replicated
- rescaling_grad: float32 [768], replicated
- recentring_grad: float32 [768], replicated
- expanding_grad: float32 [768, 3072], P(None, 'mp')
- priming_grad: float32 [3072], P('mp')
- shrinking_grad: float32 [3072, 768], P('mp')
- settling_grad: float32 [768], replicated
Inputs may be any that keep to these rules, and one draw needn't show every extreme that they name: Image i keeps its first counts[i] slots; the counts of all images sum to 18432, and some image keeps all 64. The 64 positions of an image are distinct cells of its 14 x 14 grid of patches.
All inputs are finite; a program needn't handle non-finite values. No bound on the sum of `counts` on one device may be relied on, other than what follows from the above.
Results may differ from a plain program's by a relative error of at most 0.025.
Values may be sent and summed in bfloat16 or wider, within the bound.
A program may use at most 192 MiB of HBM per device.

v0:
```python
from functools import partial
import jax
import jax.numpy as jnp
from jax import lax
from jax.sharding import PartitionSpec as P

HEADS = 12
HYP_HEADS = 4
GRID_SIDE = 14


def normalize(values, epsilon):
    center = values - jnp.mean(values, axis=-1, keepdims=True)
    return center * lax.rsqrt(jnp.mean(center * center, axis=-1, keepdims=True) + epsilon)


def norm_parts(values, epsilon):
    center = values - jnp.mean(values, axis=-1, keepdims=True)
    inverse = lax.rsqrt(jnp.mean(center * center, axis=-1, keepdims=True) + epsilon)
    return (center * inverse, inverse)


def norm_backward(upstream, normed_rows, inverse, gain_row):
    scaled = upstream * gain_row
    return inverse * (
        scaled
        - jnp.mean(scaled, axis=-1, keepdims=True)
        - normed_rows * jnp.mean(scaled * normed_rows, axis=-1, keepdims=True)
    )


def wave_embed(wavelengths, columns):
    halfway = columns // 2
    omegas = 10000.0 ** (-jnp.arange(halfway, dtype=jnp.float32) / halfway)
    angles = wavelengths.astype(jnp.float32)[:, None] * 0.01 * omegas[None, :]
    return jnp.concatenate([jnp.sin(angles), jnp.cos(angles)], axis=1)


def place_embed(positions, columns):
    quarter = columns // 4
    omegas = 10000.0 ** (-jnp.arange(quarter, dtype=jnp.float32) / quarter)
    across = (positions // GRID_SIDE).astype(jnp.float32)[..., None] * omegas
    upward = (positions % GRID_SIDE).astype(jnp.float32)[..., None] * omegas
    return jnp.concatenate(
        [jnp.sin(across), jnp.cos(across), jnp.sin(upward), jnp.cos(upward)], axis=-1
    )


def hyper_forward(wavelengths, relation, blending, widening, narrowing, shifting):
    highest = lax.Precision.HIGHEST
    columns = relation.shape[0]
    head_size = columns // HYP_HEADS
    embedded = wave_embed(wavelengths, columns)
    joined = jnp.dot(embedded, relation, precision=highest).reshape(
        embedded.shape[0], 3, HYP_HEADS, head_size
    )
    scores = jnp.einsum(
        "bhd,chd->hbc", joined[:, 0], joined[:, 1], precision=highest
    ) * head_size ** (-0.5)
    weights = jax.nn.softmax(scores, axis=-1)
    context = jnp.einsum("hbc,chd->bhd", weights, joined[:, 2], precision=highest).reshape(
        embedded.shape[0], columns
    )
    settled = normalize(embedded + jnp.dot(context, blending, precision=highest), 1e-05)
    widened = jax.nn.gelu(jnp.dot(settled, widening, precision=highest), approximate=False)
    hyper_out = normalize(settled + jnp.dot(widened, narrowing, precision=highest), 1e-05)
    bias_embed = jnp.dot(jnp.mean(hyper_out, axis=0), shifting, precision=highest)
    return (hyper_out, bias_embed)


def body(
    patches,
    wavelengths,
    counts,
    positions,
    relation,
    blending,
    widening,
    narrowing,
    generator,
    shifting,
    scaling,
    centring,
    attending,
    offsets,
    merging,
    lifting,
    rescaling,
    recentring,
    expanding,
    priming,
    shrinking,
    settling,
    cotangent,
):
    highest = lax.Precision.HIGHEST
    single = jnp.float32
    narrow = jnp.bfloat16
    local_rows = patches.shape[0]
    own_images = positions.shape[0]
    slot_count = positions.shape[1]
    model_width = merging.shape[1]
    local_width = merging.shape[0]
    head_size = model_width // HEADS
    local_heads = local_width // head_size
    score_scale = head_size ** (-0.5)
    my_index = lax.axis_index("mp")
    own_counts = lax.dynamic_slice_in_dim(counts, my_index * own_images, own_images)
    group_images = counts.shape[0]
    group_rows = group_images * slot_count
    hyper_params = tuple(
        (weight.astype(single) for weight in (relation, blending, widening, narrowing, shifting))
    )
    (hyper_out, bias_embed), hyper_pullback = jax.vjp(
        partial(hyper_forward, wavelengths), *hyper_params
    )
    hyper_low = hyper_out.astype(narrow)
    kernel_part = jnp.einsum(
        "ch,phd->pcd", hyper_low, generator, preferred_element_type=single
    ).astype(narrow)
    piece_rows = kernel_part.shape[0] * kernel_part.shape[1]
    kernel_whole = lax.all_gather(
        kernel_part.reshape(piece_rows, model_width), ("dp", "mp"), axis=0, tiled=True
    )
    embedded = jnp.dot(patches, kernel_whole, preferred_element_type=single)
    kept_rows = (
        (jnp.arange(slot_count)[None, :] < own_counts[:, None])
        .astype(single)
        .reshape(local_rows, 1)
    )
    start_rows = (
        place_embed(positions, model_width).reshape(local_rows, model_width) + bias_embed + embedded
    )
    first_hat, first_inverse = norm_parts(start_rows, 1e-06)
    first_normed = (first_hat * scaling.astype(single) + centring.astype(single)).astype(narrow)
    first_all = lax.all_gather(first_normed, "mp", axis=0, tiled=True)
    attend_flat = attending.reshape(model_width, 3 * local_width)
    attend_bias = jnp.concatenate(
        [offsets[0].astype(single), jnp.zeros((local_width,), single), offsets[1].astype(single)]
    )
    joined = (jnp.dot(first_all, attend_flat, preferred_element_type=single) + attend_bias).astype(
        narrow
    )
    split_shape = (group_images, slot_count, local_heads, head_size)
    queries = joined[:, :local_width].reshape(split_shape)
    keys_all = joined[:, local_width : 2 * local_width].reshape(split_shape)
    values = joined[:, 2 * local_width :].reshape(split_shape)
    keys_valid = (jnp.arange(slot_count)[None, :] < counts[:, None])[:, None, None, :]

    def score_block(query_rows, key_rows):
        raw_scores = (
            jnp.einsum("ishd,ithd->ihst", query_rows, key_rows, preferred_element_type=single)
            * score_scale
        )
        return jnp.where(keys_valid, raw_scores, -1000000000.0)

    scores = score_block(queries, keys_all)
    highest_score = jnp.max(scores, axis=-1, keepdims=True)
    log_total = highest_score + jnp.log(
        jnp.sum(jnp.exp(scores - highest_score), axis=-1, keepdims=True)
    )
    attention = jnp.exp(scores - log_total)
    context = (
        jnp.einsum(
            "ihst,ithd->ishd", attention.astype(narrow), values, preferred_element_type=single
        )
        .astype(narrow)
        .reshape(group_rows, local_width)
    )
    attended = lax.psum_scatter(
        jnp.dot(context, merging, preferred_element_type=single).astype(jnp.bfloat16),
        "mp",
        scatter_dimension=0,
        tiled=True,
    ).astype(jnp.float32)
    middle = start_rows + attended + lifting.astype(single)
    second_hat, second_inverse = norm_parts(middle, 1e-06)
    second_normed = (second_hat * rescaling.astype(single) + recentring.astype(single)).astype(
        narrow
    )
    second_all = lax.all_gather(second_normed, "mp", axis=0, tiled=True)
    widened = jnp.dot(second_all, expanding, preferred_element_type=single) + priming.astype(single)
    hidden = jax.nn.gelu(widened, approximate=False).astype(narrow)
    shrunk = lax.psum_scatter(
        jnp.dot(hidden, shrinking, preferred_element_type=single).astype(jnp.bfloat16),
        "mp",
        scatter_dimension=0,
        tiled=True,
    ).astype(jnp.float32)
    result = middle + shrunk + settling.astype(single)
    layer_out = (result * kept_rows).astype(narrow)
    out_grad = cotangent.astype(single) * kept_rows
    settling_grad = jnp.sum(out_grad, axis=0)
    out_all = lax.all_gather(out_grad.astype(narrow), "mp", axis=0, tiled=True)
    shrinking_grad = jnp.einsum("gf,gd->fd", hidden, out_all, preferred_element_type=single)
    hidden_grad = jnp.einsum("gd,fd->gf", out_all, shrinking, preferred_element_type=single)
    gelu_pullback = jax.vjp(partial(jax.nn.gelu, approximate=False), widened)[1]
    widened_grad = gelu_pullback(hidden_grad)[0].astype(narrow)
    priming_grad = jnp.sum(widened_grad, axis=0, dtype=single)
    expanding_grad = jnp.einsum(
        "gd,gf->df", second_all, widened_grad, preferred_element_type=single
    )
    second_grad = lax.psum_scatter(
        jnp.einsum("gf,df->gd", widened_grad, expanding, preferred_element_type=single).astype(
            jnp.bfloat16
        ),
        "mp",
        scatter_dimension=0,
        tiled=True,
    ).astype(jnp.float32)
    rescaling_grad = jnp.sum(second_grad * second_hat, axis=0)
    recentring_grad = jnp.sum(second_grad, axis=0)
    middle_grad = out_grad + norm_backward(
        second_grad, second_hat, second_inverse, rescaling.astype(single)
    )
    lifting_grad = jnp.sum(middle_grad, axis=0)
    middle_all = lax.all_gather(middle_grad.astype(narrow), "mp", axis=0, tiled=True)
    merging_grad = jnp.einsum("gc,gd->cd", context, middle_all, preferred_element_type=single)
    context_grad = (
        jnp.einsum("gd,cd->gc", middle_all, merging, preferred_element_type=single)
        .astype(narrow)
        .reshape(split_shape)
    )
    attention = jnp.exp(score_block(queries, keys_all) - log_total)
    attention_grad = jnp.einsum(
        "ishd,ithd->ihst", context_grad, values, preferred_element_type=single
    )
    values_grad = jnp.einsum(
        "ihst,ishd->ithd", attention.astype(narrow), context_grad, preferred_element_type=single
    ).astype(narrow)
    scores_grad = (
        attention * (attention_grad - jnp.sum(attention * attention_grad, axis=-1, keepdims=True))
    ).astype(narrow)
    queries_grad = (
        jnp.einsum("ihst,ithd->ishd", scores_grad, keys_all, preferred_element_type=single)
        * score_scale
    ).astype(narrow)
    keys_grad = (
        jnp.einsum("ihst,ishd->ithd", scores_grad, queries, preferred_element_type=single)
        * score_scale
    ).astype(narrow)
    joined_grad = jnp.concatenate(
        [
            queries_grad.reshape(group_rows, local_width),
            keys_grad.reshape(group_rows, local_width),
            values_grad.reshape(group_rows, local_width),
        ],
        axis=1,
    )
    attending_grad = jnp.einsum(
        "gd,gc->dc", first_all, joined_grad, preferred_element_type=single
    ).reshape(model_width, 3, local_width)
    offsets_grad = jnp.stack(
        [
            jnp.sum(joined_grad[:, :local_width], axis=0, dtype=single),
            jnp.sum(joined_grad[:, 2 * local_width :], axis=0, dtype=single),
        ]
    )
    first_grad = lax.psum_scatter(
        jnp.einsum("gc,dc->gd", joined_grad, attend_flat, preferred_element_type=single).astype(
            jnp.bfloat16
        ),
        "mp",
        scatter_dimension=0,
        tiled=True,
    ).astype(jnp.float32)
    scaling_grad = jnp.sum(first_grad * first_hat, axis=0)
    centring_grad = jnp.sum(first_grad, axis=0)
    start_grad = middle_grad + norm_backward(
        first_grad, first_hat, first_inverse, scaling.astype(single)
    )
    shift_total = jnp.sum(start_grad, axis=0)
    start_low = start_grad.astype(narrow)
    patches_grad = jnp.einsum("rd,kd->rk", start_low, kernel_whole, preferred_element_type=single)
    kernel_grad = lax.psum_scatter(
        jnp.einsum("rk,rd->kd", patches, start_low, preferred_element_type=single),
        ("dp", "mp"),
        scatter_dimension=0,
        tiled=True,
    ).reshape(kernel_part.shape)
    generator_grad = jnp.einsum(
        "ch,pcd->phd", hyper_low.astype(single), kernel_grad, precision=highest
    )
    hyper_part = jnp.einsum("pcd,phd->ch", kernel_grad, generator.astype(single), precision=highest)
    (
        scaling_grad,
        centring_grad,
        rescaling_grad,
        recentring_grad,
        lifting_grad,
        settling_grad,
        shift_total,
        hyper_part,
    ) = lax.psum(
        (
            scaling_grad,
            centring_grad,
            rescaling_grad,
            recentring_grad,
            lifting_grad,
            settling_grad,
            shift_total,
            hyper_part,
        ),
        ("dp", "mp"),
    )
    relation_grad, blending_grad, widening_grad, narrowing_grad, shifting_grad = hyper_pullback(
        (hyper_part, shift_total)
    )
    attending_grad, offsets_grad, merging_grad, expanding_grad, priming_grad, shrinking_grad = (
        lax.psum(
            (
                attending_grad,
                offsets_grad,
                merging_grad,
                expanding_grad,
                priming_grad,
                shrinking_grad,
            ),
            "dp",
        )
    )
    return (
        layer_out,
        patches_grad,
        relation_grad,
        blending_grad,
        widening_grad,
        narrowing_grad,
        generator_grad,
        shifting_grad,
        scaling_grad,
        centring_grad,
        attending_grad,
        offsets_grad,
        merging_grad,
        lifting_grad,
        rescaling_grad,
        recentring_grad,
        expanding_grad,
        priming_grad,
        shrinking_grad,
        settling_grad,
    )


def solution(mesh):
    placed = (
        P(("dp", "mp"), None),
        P(),
        P("dp"),
        P(("dp", "mp"), None),
        P(),
        P(),
        P(),
        P(),
        P(("dp", "mp"), None, None),
        P(),
        P(),
        P(),
        P(None, None, "mp"),
        P(None, "mp"),
        P("mp", None),
        P(),
        P(),
        P(),
        P(None, "mp"),
        P("mp"),
        P("mp", None),
        P(),
        P(("dp", "mp"), None),
    )
    return jax.shard_map(
        body,
        mesh=mesh,
        in_specs=placed,
        out_specs=(
            P(("dp", "mp"), None),
            P(("dp", "mp"), None),
            P(),
            P(),
            P(),
            P(),
            P(("dp", "mp"), None, None),
            P(),
            P(),
            P(),
            P(None, None, "mp"),
            P(None, "mp"),
            P("mp", None),
            P(),
            P(),
            P(),
            P(None, "mp"),
            P("mp"),
            P("mp", None),
            P(),
        ),
        check_vma=False,
    )
```

profile of v0, /device:TPU:0, one launch (start us, length us, event | category | flops | bytes accessed | tf_op | source)
XLA Modules:
  0.0 1249.0 jit_solution(4035318917937270795)
XLA Ops:
  18.8 5.0 multiply_sine_fusion.1
  23.8 60.3 %all-gather.6.cloned.1.call-done = bf16[3072,768]{1,0:T(8,128)(2,1)} async-done(((bf16[96,768]{1,0:T(8,128)(2,1)}), bf16[3072,768]{1,0:T(8,128)(2,1)}) %all-gather.6.cloned.1.call-update) | async-done | bytes 4718608 | tf_op jit(solution)/shard_map/all_gather | solution.py:122
  84.1 7.9 fusion.111
  96.2 87.1 %all-gather.8.cloned.1.call-done = bf16[3072,768]{0,1:T(8,128)(2,1)} async-done(((bf16[768,768]{0,1:T(8,128)(2,1)}), bf16[3072,768]{0,1:T(8,128)(2,1)}) %all-gather.8.cloned.1.call-update) | async-done | bytes 4718608 | tf_op jit(solution)/shard_map/all_gather | solution.py:136
  183.3 5.5 add_convert_fusion.1
  190.4 4.2 reshape.283
  194.6 4.2 reshape.284
  198.8 4.8 copy.108
  206.4 4.8 copy.117
  211.2 3.9 fusion.6
  223.5 3.4 reshape.285
  226.9 3.6 convolution_convert_fusion.3
  231.3 83.2 %reduce-scatter.8.cloned.1.call-done = bf16[768,768]{0,1:T(8,128)(2,1)} async-done(((bf16[3072,768]{0,1:T(8,128)(2,1)}), bf16[768,768]{0,1:T(8,128)(2,1)}) %reduce-scatter.8.cloned.1.call-update) | async-done | bytes 1179664 | tf_op jit(solution)/shard_map/reduce_scatter | solution.py:170
  322.8 86.9 %all-gather.10.cloned.1.call-done = bf16[3072,768]{0,1:T(8,128)(2,1)} async-done(((bf16[768,768]{0,1:T(8,128)(2,1)}), bf16[3072,768]{0,1:T(8,128)(2,1)}) %all-gather.10.cloned.1.call-update) | async-done | bytes 4718608 | tf_op jit(solution)/shard_map/all_gather | solution.py:181
  409.7 10.7 fusion.112
  420.4 79.2 %all-gather.12.cloned.1.call-done = bf16[3072,768]{0,1:T(8,128)(2,1)} async-done(((bf16[768,768]{0,1:T(8,128)(2,1)}), bf16[3072,768]{0,1:T(8,128)(2,1)}) %all-gather.12.cloned.1.call-update) | async-done | bytes 4718608 | tf_op jit(solution)/shard_map/all_gather | solution.py:194
  499.5 28.5 %convert_reduce_fusion = (f32[768]{0:T(1024)S(1)}, bf16[3072,768]{1,0:T(8,128)(2,1)S(1)}, f32[3072,768]{1,0:T(8,128)}) fusion(f32[3072,768]{1,0:T(8,128)} %fusion.112, f32[768]{0:T(1024)S(1)} %convert_element_type.192, bf16[3072,768]{0,1:T(8,128)(2,1)} %all-gather.12.cloned.1.call-done, bf16[768,768]{1,0:T(8,128)(2,1)} %param.43), kind=kOutput, calls=%fused_computation.2 | convolution fusion | flops 3800825088 | bytes 29497344 | tf_op jit(solution)/shard_map/gd,fd->gf/dot_general | solution.py:196
  530.1 5.5 convolution_convert_fusion
  536.0 10.8 multiply_convert_fusion
  546.8 8.8 convolution_convert_fusion.1
  556.2 63.3 %reduce-scatter.12.cloned.1.call-done = bf16[768,768]{0,1:T(8,128)(2,1)} async-done(((bf16[3072,768]{0,1:T(8,128)(2,1)}), bf16[768,768]{0,1:T(8,128)(2,1)}) %reduce-scatter.12.cloned.1.call-update) | async-done | bytes 1179664 | tf_op jit(solution)/shard_map/reduce_scatter | solution.py:203
  622.6 85.7 %reduce-scatter.10.cloned.1.call-done = bf16[768,768]{0,1:T(8,128)(2,1)} async-done(((bf16[3072,768]{0,1:T(8,128)(2,1)}), bf16[768,768]{0,1:T(8,128)(2,1)}) %reduce-scatter.10.cloned.1.call-update) | async-done | bytes 1179664 | tf_op jit(solution)/shard_map/reduce_scatter | solution.py:184
  708.2 4.3 fusion.101
  715.1 90.0 %all-gather.14.cloned.1.call-done = bf16[3072,768]{0,1:T(8,128)(2,1)} async-done(((bf16[768,768]{0,1:T(8,128)(2,1)}), bf16[3072,768]{0,1:T(8,128)(2,1)}) %all-gather.14.cloned.1.call-update) | async-done | bytes 4718608 | tf_op jit(solution)/shard_map/all_gather | solution.py:217
  805.1 3.4 convolution_convert_fusion.4
  811.7 4.9 copy.116
  816.6 5.5 convert_reduce_fusion.1
  833.1 4.6 copy.124
  837.7 3.4 reshape.288
  841.0 4.6 copy.120
  845.6 4.3 reshape.287
  852.3 4.6 copy.126
  856.9 4.3 reshape.289
  864.6 7.5 convolution_convert_fusion.2
  872.4 83.6 %reduce-scatter.14.cloned.1.call-done = bf16[768,768]{0,1:T(8,128)(2,1)} async-done(((bf16[3072,768]{0,1:T(8,128)(2,1)}), bf16[768,768]{0,1:T(8,128)(2,1)}) %reduce-scatter.14.cloned.1.call-update) | async-done | bytes 1179664 | tf_op jit(solution)/shard_map/reduce_scatter | solution.py:259
  963.1 8.5 convolution_bitcast_fusion
  971.6 9.6 copy.144
  982.0 9.0 fusion.115
  991.0 9.5 fusion.116
  1003.1 14.6 %all-reduce.4 = (f32[2,192]{1,0:T(2,128)}, f32[768]{0:T(1024)}) all-reduce(f32[2,192]{1,0:T(2,128)S(1)} %pad_maximum_fusion.2, f32[768]{0:T(1024)S(1)} %get-tuple-element.102), channel_id=1, replica_groups=mesh['dp'=8,'mp'=4] {'dp'}, use_global_device_ids=true, to_apply=%region_38.39 | all-reduce | flops 1152 | bytes 9216 | tf_op jit(solution)/shard_map/psum | solution.py:311
  1017.7 5.2 fusion.114
  1022.9 6.6 fusion.113
  1030.8 8.8 fusion.35
  1039.7 78.7 %reduce-scatter.16.cloned.1.call-done = f32[96,768]{1,0:T(8,128)} async-done(((f32[3072,768]{1,0:T(8,128)}), f32[96,768]{1,0:T(8,128)}) %reduce-scatter.16.cloned.1.call-update) | async-done | bytes 294928 | tf_op jit(solution)/shard_map/reduce_scatter | solution.py:275
  1120.7 41.7 %all-reduce.3 = (f32[12,128]{1,0:T(8,128)S(1)}, f32[768]{0:T(1024)S(1)}, f32[768]{0:T(1024)}, f32[768]{0:T(1024)}, f32[768]{0:T(1024)}, /*index=5*/f32[768]{0:T(1024)}, f32[768]{0:T(1024)}, f32[768]{0:T(1024)}) all-reduce(f32[12,128]{1,0:T(8,128)S(1)} %convolution_bitcast_fusion.6, ...), channel_id=1, replica_groups=mesh['dp'=8,'mp'=4] {'dp','mp'}, use_global_device_ids=true, to_apply=%region_23.24 | all-reduce | flops 6912 | bytes 55296 | tf_op jit(solution)/shard_map/psum | solution.py:294
  1167.1 4.3 convolution_bitcast_fusion.1
  1171.4 3.6 copy.133
  1183.0 52.6 %all-reduce.8.cloned.1.call-done = (f32[768,3,192]{0,2,1:T(8,128)}, f32[192,768]{1,0:T(8,128)}, f32[768,768]{1,0:T(8,128)}, f32[768,768]{1,0:T(8,128)}) async-done(((f32[768,3,192]{0,2,1:T(8,128)}, f32[192,768]{1,0:T(8,128)}, f32[768,768]{1,0:T(8,128)}, f32[768,768]{1,0:T(8,128)}), (f32[768,3,192]{0,2,1:T(8,128)}, f32[192,768]{1,0:T(8,128)}, f32[768,768]{1,0:T(8,128)}, ...) | async-done | bytes 7077904 | tf_op jit(solution)/shard_map/psum | solution.py:311
  (305 shorter events, 98.8 us)
Async XLA Ops:
  7.2 9.3 copy-start
  7.2 76.9 %all-gather.6.cloned.1.call-start = ((), (), s32[]{:S(2)}) async-start(), calls=%async_computation.5 | async-start | bytes 4866048 | tf_op jit(solution)/shard_map/all_gather | solution.py:122
  8.0 9.6 copy-start.67
  8.2 9.5 copy-start.68
  8.2 9.5 copy-start.59
  8.2 10.3 copy-start.20
  17.6 165.6 %all-gather.8.cloned.1.call-start = ((), (), s32[]{:S(2)}) async-start(), calls=%async_computation.6 | async-start | bytes 5898240 | tf_op jit(solution)/shard_map/all_gather | solution.py:136
  17.7 74.7 %copy-start.46 = (f32[768]{0:T(1024)}, f32[768]{0:T(1024)S(1)}, u32[]{:S(2)}) copy-start(f32[768]{0:T(1024)S(1)} %convert_element_type.175) | copy-start | bytes 9220
  92.0 91.2 %copy-start.80 = (bf16[768,3,192]{0,2,1:T(8,128)(2,1)S(1)}, bf16[768,3,192]{0,2,1:T(8,128)(2,1)}, u32[]{:S(2)}) copy-start(bf16[768,3,192]{0,2,1:T(8,128)(2,1)} %param.35) | copy-start | bytes 2654212
  95.4 219.0 %reduce-scatter.8.cloned.1.call-start = ((), (), s32[]{:S(2)}) async-start(), calls=%async_computation.7 | async-start | bytes 5898240 | tf_op jit(solution)/shard_map/reduce_scatter | solution.py:170
  215.1 5.5 copy-start.1
  220.6 6.3 copy-start.17
  230.6 179.1 %all-gather.10.cloned.1.call-start = ((), (), s32[]{:S(2)}) async-start(), calls=%async_computation.8 | async-start | bytes 5898240 | tf_op jit(solution)/shard_map/all_gather | solution.py:181
  319.6 179.9 %all-gather.12.cloned.1.call-start = ((), (), s32[]{:S(2)}) async-start(), calls=%async_computation.10 | async-start | bytes 5898240 | tf_op jit(solution)/shard_map/all_gather | solution.py:194
  322.8 296.8 %reduce-scatter.12.cloned.1.call-start = ((), (), s32[]{:S(2)}) async-start(), calls=%async_computation.11 | async-start | bytes 5898240 | tf_op jit(solution)/shard_map/reduce_scatter | solution.py:203
  499.5 30.6 %copy-start.79 = (bf16[768,768]{1,0:T(8,128)(2,1)S(1)}, bf16[768,768]{1,0:T(8,128)(2,1)}, u32[]{:S(2)}) copy-start(bf16[768,768]{1,0:T(8,128)(2,1)} %param.41) | copy-start | bytes 3538948
  535.7 172.6 %reduce-scatter.10.cloned.1.call-start = ((), (), s32[]{:S(2)}) async-start(), calls=%async_computation.9 | async-start | bytes 5898240 | tf_op jit(solution)/shard_map/reduce_scatter | solution.py:184
  555.6 249.6 %all-gather.14.cloned.1.call-start = ((), (), s32[]{:S(2)}) async-start(), calls=%async_computation.12 | async-start | bytes 5898240 | tf_op jit(solution)/shard_map/all_gather | solution.py:217
  715.1 241.0 %reduce-scatter.14.cloned.1.call-start = ((), (), s32[]{:S(2)}) async-start(), calls=%async_computation.13 | async-start | bytes 5898240 | tf_op jit(solution)/shard_map/reduce_scatter | solution.py:259
  811.7 10.4 slice-start
  816.6 5.5 slice-start.1
  816.6 5.7 copy-start.6
  816.6 6.6 copy-start.10
  872.2 83.9 %copy-start.43 = (f32[768]{0:T(1024)S(1)}, f32[768]{0:T(1024)}, u32[]{:S(2)}) copy-start(f32[768]{0:T(1024)} %copy-done.42) | copy-start | bytes 9220
  872.2 83.9 %copy-start.47 = (f32[768]{0:T(1024)S(1)}, f32[768]{0:T(1024)}, u32[]{:S(2)}) copy-start(f32[768]{0:T(1024)} %copy-done.46) | copy-start | bytes 9220
  872.2 83.9 %copy-start.49 = (f32[768]{0:T(1024)S(1)}, f32[768]{0:T(1024)}, u32[]{:S(2)}) copy-start(f32[768]{0:T(1024)} %copy-done.48) | copy-start | bytes 9220
  872.2 246.2 %reduce-scatter.16.cloned.1.call-start = ((), (), s32[]{:S(2)}) async-start(), calls=%async_computation.14 | async-start | bytes 9732096 | tf_op jit(solution)/shard_map/reduce_scatter | solution.py:275
  981.3 254.3 %all-reduce.8.cloned.1.call-start = ((), (), s32[]{:S(2)}) async-start(), calls=%async_computation.15 | async-start | bytes 14155776 | tf_op jit(solution)/shard_map/psum | solution.py:311
  990.9 26.7 %copy-start.12 = (bf16[3072,192]{0,1:T(8,128)(2,1)S(1)}, bf16[3072,192]{0,1:T(8,128)(2,1)}, u32[]{:S(2)}) copy-start(bf16[3072,192]{0,1:T(8,128)(2,1)} %copy-done.11) | copy-start | bytes 3538948
  1017.7 5.2 copy-start.23
  1030.7 131.7 %copy-start.21 = (bf16[128,768]{1,0:T(8,128)(2,1)S(1)}, bf16[128,768]{1,0:T(8,128)(2,1)}, u32[]{:S(2)}) copy-start(bf16[128,768]{1,0:T(8,128)(2,1)} %param.32) | copy-start | bytes 589828
  1030.7 131.9 %copy-start.25 = (f32[12,128]{1,0:T(8,128)S(1)}, f32[12,128]{1,0:T(8,128)}, u32[]{:S(2)}) copy-start(f32[12,128]{1,0:T(8,128)} %copy-done.24) | copy-start | bytes 18436
  1030.7 131.9 %copy-start.54 = (f32[12]{0:T(128)S(1)}, f32[12]{0:T(128)}, u32[]{:S(2)}) copy-start(f32[12]{0:T(128)} %copy-done.53) | copy-start | bytes 148
  1030.7 132.1 %copy-start.77 = (f32[12]{0:T(128)S(1)}, f32[12]{0:T(128)}, u32[]{:S(2)}) copy-start(f32[12]{0:T(128)} %copy-done.76) | copy-start | bytes 148
  1030.7 132.2 %copy-start.58 = (f32[12]{0:T(128)S(1)}, f32[12]{0:T(128)}, u32[]{:S(2)}) copy-start(f32[12]{0:T(128)} %copy-done.57) | copy-start | bytes 148
  1030.8 132.4 %copy-start.37 = (f32[12,2048]{1,0:T(8,128)S(1)}, f32[12,2048]{1,0:T(8,128)}, u32[]{:S(2)}) copy-start(f32[12,2048]{1,0:T(8,128)} %copy-done.36) | copy-start | bytes 294916
  1039.6 125.3 %copy-start.16 = (bf16[128,2048]{1,0:T(8,128)(2,1)S(1)}, bf16[128,2048]{1,0:T(8,128)(2,1)}, u32[]{:S(2)}) copy-start(bf16[128,2048]{1,0:T(8,128)(2,1)} %param.29) | copy-start | bytes 1572868
  1039.6 125.3 %copy-start.27 = (f32[12,128]{1,0:T(8,128)S(1)}, f32[12,128]{1,0:T(8,128)}, u32[]{:S(2)}) copy-start(f32[12,128]{1,0:T(8,128)} %copy-done.26) | copy-start | bytes 18436
  1039.6 125.3 %copy-start.56 = (f32[12]{0:T(128)S(1)}, f32[12]{0:T(128)}, u32[]{:S(2)}) copy-start(f32[12]{0:T(128)} %copy-done.55) | copy-start | bytes 148
  1039.6 126.0 %copy-start.75 = (f32[12]{0:T(128)S(1)}, f32[12]{0:T(128)}, u32[]{:S(2)}) copy-start(f32[12]{0:T(128)} %copy-done.74) | copy-start | bytes 148
  1039.6 126.0 %copy-start.63 = (f32[12]{0:T(128)S(1)}, f32[12]{0:T(128)}, u32[]{:S(2)}) copy-start(f32[12]{0:T(128)} %copy-done.62) | copy-start | bytes 148
  1039.6 126.2 %copy-start.50 = (bf16[128,128]{1,0:T(8,128)(2,1)S(1)}, bf16[128,128]{1,0:T(8,128)(2,1)}, u32[]{:S(2)}) copy-start(bf16[128,128]{1,0:T(8,128)(2,1)} %param.28) | copy-start | bytes 98308
  1039.6 126.5 %copy-start.29 = (f32[4,12,12]{1,2,0:T(8,128)S(1)}, f32[4,12,12]{1,2,0:T(8,128)}, u32[]{:S(2)}) copy-start(f32[4,12,12]{1,2,0:T(8,128)} %copy-done.28) | copy-start | bytes 6916
  1039.6 126.5 %copy-start.35 = (f32[12,1,4,32]{3,2,1,0:T(4,128)S(1)}, f32[12,1,4,32]{3,2,1,0:T(4,128)}, u32[]{:S(2)}) copy-start(f32[12,1,4,32]{3,2,1,0:T(4,128)} %copy-done.34) | copy-start | bytes 18436
  1039.6 126.5 %copy-start.52 = (f32[4,12]{1,0:T(4,128)S(1)}, f32[4,12]{1,0:T(4,128)}, u32[]{:S(2)}) copy-start(f32[4,12]{1,0:T(4,128)} %copy-done.51) | copy-start | bytes 580
  1119.4 47.1 %copy-start.33 = (f32[12,1,4,32]{3,2,1,0:T(4,128)S(1)}, f32[12,1,4,32]{3,2,1,0:T(4,128)}, u32[]{:S(2)}) copy-start(f32[12,1,4,32]{3,2,1,0:T(4,128)} %copy-done.32) | copy-start | bytes 18436
  1119.4 47.4 %copy-start.31 = (f32[12,1,4,32]{3,2,1,0:T(4,128)S(1)}, f32[12,1,4,32]{3,2,1,0:T(4,128)}, u32[]{:S(2)}) copy-start(f32[12,1,4,32]{3,2,1,0:T(4,128)} %copy-done.30) | copy-start | bytes 18436
  1171.4 4.6 copy-start.41
  (48 other events, 103.4 us)
Sparse Core Ops, SparseCore 0:
  17.7 66.2 all-gather.5
  95.5 87.6 all-gather.7
  230.7 83.6 reduce-scatter.7
  319.8 89.8 all-gather.9
  411.7 87.7 all-gather.11
  535.8 83.6 reduce-scatter.11
  622.4 85.7 reduce-scatter.9
  715.2 89.9 all-gather.13
  872.3 83.6 reduce-scatter.13
  981.4 136.9 reduce-scatter.15
  1123.2 112.3 all-reduce.7
where the time goes:
time: 1260 us; the launch traced here: 1250 us
  waiting for transfers between devices  851 us (68%)
  matrix products  171 us (14%)
  local copies, waits for them, and re-layouts  110 us (9%)
  blocking collectives  56.3 us (4%)
  other arithmetic  44.2 us (4%)
  between operations  15.2 us (1%)
    all_gather x1, waiting for transfers between devices, body(): lax.all_gather(middle_grad.astype(narrow), 'mp', axis=0, tiled=True)  90 us
    all_gather x1, waiting for transfers between devices, body(): first_all = lax.all_gather(first_normed, 'mp', axis=0, tiled=True)  87.1 us
    all_gather x1, waiting for transfers between devices, body(): second_all = lax.all_gather(second_normed, 'mp', axis=0, tiled=True)  86.9 us
    reduce_scatter x1, waiting for transfers between devices, body(): lax.psum_scatter(jnp.dot(hidden, shrinking, preferred_element_type=single...  85.7 us
    reduce_scatter x1, waiting for transfers between devices, body(): lax.psum_scatter(jnp.einsum('gc,dc->gd', joined_grad, attend_flat, prefer...  83.6 us
    reduce_scatter x1, waiting for transfers between devices, body(): lax.psum_scatter(jnp.dot(context, merging, preferred_element_type=single)...  83.2 us
    all_gather x1, waiting for transfers between devices, body(): out_all = lax.all_gather(out_grad.astype(narrow), 'mp', axis=0, tiled=True)  79.2 us
    reduce_scatter x1, waiting for transfers between devices, body(): lax.psum_scatter(jnp.einsum('rk,rd->kd', patches, start_low, preferred_el...  78.7 us
  transfers between devices with their start and end apart: 11, of which 11 were waited for; matrix products, arithmetic and copies ran while one was open for 9% of the time, Pallas kernels for 0%

commit v1 on v0

--- a/solution.py
+++ b/solution.py
@@ -133,7 +133,14 @@
     )
     first_hat, first_inverse = norm_parts(start_rows, 1e-06)
     first_normed = (first_hat * scaling.astype(single) + centring.astype(single)).astype(narrow)
-    first_all = lax.all_gather(first_normed, "mp", axis=0, tiled=True)
+    ways, here = (lax.axis_size("mp"), lax.axis_index("mp"))
+    first_all, reach = (first_normed, 1)
+    while reach < ways:
+        theirs = lax.ppermute(first_all, "mp", [(d, d ^ reach) for d in range(ways)])
+        mine_first = jnp.concatenate([first_all, theirs], axis=0)
+        theirs_first = jnp.concatenate([theirs, first_all], axis=0)
+        first_all = jnp.where(here & reach == 0, mine_first, theirs_first)
+        reach = 2 * reach
     attend_flat = attending.reshape(model_width, 3 * local_width)
     attend_bias = jnp.concatenate(
         [offsets[0].astype(single), jnp.zeros((local_width,), single), offsets[1].astype(single)]

time: 1260 us -> 1310 us (1.040)
  waiting for transfers between devices: 851 us -> 889 us
    ppermute x0 -> x2, waiting for transfers between devices: none -> 129 us  [body(): lax.ppermute(first_all, 'mp', [(d, d ^ reach) for d in range(ways)])]
    all_gather x1 -> x0, waiting for transfers between devices: 87.1 us -> none  [body(): first_all = lax.all_gather(first_normed, 'mp', axis=0, tiled=True)]
    unnamed x180 -> x178, local copies, waits for them, and re-layouts: 42.6 us -> 42.2 us
  transfers between devices with their start and end apart: 11 -> 12, of which waited for: 11 -> 12; matrix products, arithmetic and copies ran while one was open for 9% -> 8% of each run, Pallas kernels for 0% -> 0%
where the time goes in v1:
time: 1310 us; the launch traced here: 1300 us
  waiting for transfers between devices  889 us (68%)
  matrix products  175 us (13%)
  local copies, waits for them, and re-layouts  110 us (8%)
  blocking collectives  56.4 us (4%)
  other arithmetic  46.5 us (4%)
  between operations  15.4 us (1%)
    ppermute x2, waiting for transfers between devices, body(): lax.ppermute(first_all, 'mp', [(d, d ^ reach) for d in range(ways)])  129 us
    all_gather x1, waiting for transfers between devices, body(): lax.all_gather(middle_grad.astype(narrow), 'mp', axis=0, tiled=True)  90 us
    all_gather x1, waiting for transfers between devices, body(): second_all = lax.all_gather(second_normed, 'mp', axis=0, tiled=True)  86.7 us
    reduce_scatter x1, waiting for transfers between devices, body(): lax.psum_scatter(jnp.dot(hidden, shrinking, preferred_element_type=single...  85.5 us
    reduce_scatter x1, waiting for transfers between devices, body(): lax.psum_scatter(jnp.einsum('gc,dc->gd', joined_grad, attend_flat, prefer...  83.6 us
    reduce_scatter x1, waiting for transfers between devices, body(): lax.psum_scatter(jnp.dot(context, merging, preferred_element_type=single)...  83.1 us
    all_gather x1, waiting for transfers between devices, body(): out_all = lax.all_gather(out_grad.astype(narrow), 'mp', axis=0, tiled=True)  79.2 us
    reduce_scatter x1, waiting for transfers between devices, body(): lax.psum_scatter(jnp.einsum('rk,rd->kd', patches, start_low, preferred_el...  75.9 us
  transfers between devices with their start and end apart: 12, of which 12 were waited for; matrix products, arithmetic and copies ran while one was open for 8% of the time, Pallas kernels for 0%

profile of v1, /device:TPU:0, one launch (start us, length us, event | category | flops | bytes accessed | tf_op | source)
XLA Modules:
  0.0 1296.4 jit_solution(1468726410651737585)
XLA Ops:
  18.8 5.0 multiply_sine_fusion.1
  23.8 60.3 %all-gather.5.cloned.1.call-done = bf16[3072,768]{1,0:T(8,128)(2,1)} async-done(((bf16[96,768]{1,0:T(8,128)(2,1)}), bf16[3072,768]{1,0:T(8,128)(2,1)}) %all-gather.5.cloned.1.call-update) | async-done | bytes 4718608 | tf_op jit(solution)/shard_map/all_gather | solution.py:122
  84.1 7.9 fusion.114
  95.3 26.8 %collective-permute-done = bf16[768,768]{0,1:T(8,128)(2,1)} collective-permute-done((bf16[768,768]{0,1:T(8,128)(2,1)S(1)}, bf16[768,768]{0,1:T(8,128)(2,1)}, u32[]{:S(2)}, u32[]{:S(2)}) %collective-permute-start) | collective-permute-done | bytes 1179680 | tf_op jit(solution)/shard_map/ppermute | solution.py:139
  127.2 102.5 %collective-permute-done.1 = bf16[1536,768]{0,1:T(8,128)(2,1)} collective-permute-done((bf16[1536,768]{0,1:T(8,128)(2,1)}, bf16[1536,768]{0,1:T(8,128)(2,1)}, u32[]{:S(2)}, u32[]{:S(2)}) %collective-permute-start.1) | collective-permute-done | bytes 2359328 | tf_op jit(solution)/shard_map/ppermute | solution.py:139
  229.8 7.0 add_convert_fusion.1
  238.4 4.2 reshape.283
  242.7 4.2 reshape.284
  246.9 4.8 copy.108
  254.6 4.8 copy.117
  259.4 3.9 fusion.6
  271.7 3.4 reshape.285
  275.1 3.6 convolution_convert_fusion.3
  279.4 83.1 %reduce-scatter.8.cloned.1.call-done = bf16[768,768]{0,1:T(8,128)(2,1)} async-done(((bf16[3072,768]{0,1:T(8,128)(2,1)}), bf16[768,768]{0,1:T(8,128)(2,1)}) %reduce-scatter.8.cloned.1.call-update) | async-done | bytes 1179664 | tf_op jit(solution)/shard_map/reduce_scatter | solution.py:177
  371.1 86.7 %all-gather.7.cloned.1.call-done = bf16[3072,768]{0,1:T(8,128)(2,1)} async-done(((bf16[768,768]{0,1:T(8,128)(2,1)}), bf16[3072,768]{0,1:T(8,128)(2,1)}) %all-gather.7.cloned.1.call-update) | async-done | bytes 4718608 | tf_op jit(solution)/shard_map/all_gather | solution.py:188
  457.8 10.7 fusion.115
  468.4 79.2 %all-gather.9.cloned.1.call-done = bf16[3072,768]{0,1:T(8,128)(2,1)} async-done(((bf16[768,768]{0,1:T(8,128)(2,1)}), bf16[3072,768]{0,1:T(8,128)(2,1)}) %all-gather.9.cloned.1.call-update) | async-done | bytes 4718608 | tf_op jit(solution)/shard_map/all_gather | solution.py:201
  547.6 28.5 %convert_reduce_fusion = (f32[768]{0:T(1024)S(1)}, bf16[3072,768]{1,0:T(8,128)(2,1)S(1)}, f32[3072,768]{1,0:T(8,128)}) fusion(f32[3072,768]{1,0:T(8,128)} %fusion.115, f32[768]{0:T(1024)S(1)} %convert_element_type.192, bf16[3072,768]{0,1:T(8,128)(2,1)} %all-gather.9.cloned.1.call-done, bf16[768,768]{1,0:T(8,128)(2,1)} %param.43), kind=kOutput, calls=%fused_computation.2 | convolution fusion | flops 3800825088 | bytes 29497344 | tf_op jit(solution)/shard_map/gd,fd->gf/dot_general | solution.py:203
  578.2 5.5 convolution_convert_fusion
  584.2 10.8 multiply_convert_fusion
  595.0 8.8 convolution_convert_fusion.1
  604.5 63.2 %reduce-scatter.12.cloned.1.call-done = bf16[768,768]{0,1:T(8,128)(2,1)} async-done(((bf16[3072,768]{0,1:T(8,128)(2,1)}), bf16[768,768]{0,1:T(8,128)(2,1)}) %reduce-scatter.12.cloned.1.call-update) | async-done | bytes 1179664 | tf_op jit(solution)/shard_map/reduce_scatter | solution.py:210
  670.7 85.5 %reduce-scatter.10.cloned.1.call-done = bf16[768,768]{0,1:T(8,128)(2,1)} async-done(((bf16[3072,768]{0,1:T(8,128)(2,1)}), bf16[768,768]{0,1:T(8,128)(2,1)}) %reduce-scatter.10.cloned.1.call-update) | async-done | bytes 1179664 | tf_op jit(solution)/shard_map/reduce_scatter | solution.py:191
  756.2 4.3 fusion.104
  763.1 90.0 %all-gather.11.cloned.1.call-done = bf16[3072,768]{0,1:T(8,128)(2,1)} async-done(((bf16[768,768]{0,1:T(8,128)(2,1)}), bf16[3072,768]{0,1:T(8,128)(2,1)}) %all-gather.11.cloned.1.call-update) | async-done | bytes 4718608 | tf_op jit(solution)/shard_map/all_gather | solution.py:224
  853.1 3.4 convolution_convert_fusion.4
  859.5 4.9 copy.116
  864.3 5.5 convert_reduce_fusion.1
  880.7 4.6 copy.124
  888.7 4.6 copy.120
  893.3 4.3 reshape.287
  900.0 4.6 copy.126
  904.6 4.3 reshape.289
  912.3 7.5 convolution_convert_fusion.2
  920.1 83.6 %reduce-scatter.14.cloned.1.call-done = bf16[768,768]{0,1:T(8,128)(2,1)} async-done(((bf16[3072,768]{0,1:T(8,128)(2,1)}), bf16[768,768]{0,1:T(8,128)(2,1)}) %reduce-scatter.14.cloned.1.call-update) | async-done | bytes 1179664 | tf_op jit(solution)/shard_map/reduce_scatter | solution.py:266
  1010.8 8.5 convolution_bitcast_fusion
  1019.3 9.7 copy.144
  1029.6 9.0 fusion.117
  1038.6 9.6 fusion.118
  1050.8 14.8 %all-reduce.4 = (f32[2,192]{1,0:T(2,128)}, f32[768]{0:T(1024)}) all-reduce(f32[2,192]{1,0:T(2,128)S(1)} %pad_maximum_fusion.2, f32[768]{0:T(1024)S(1)} %get-tuple-element.102), channel_id=1, replica_groups=mesh['dp'=8,'mp'=4] {'dp'}, use_global_device_ids=true, to_apply=%region_38.39 | all-reduce | flops 1152 | bytes 9216 | tf_op jit(solution)/shard_map/psum | solution.py:318
  1065.6 5.2 fusion.116
  1070.8 8.1 fusion.34
  1080.2 9.6 fusion.36
  1089.9 75.9 %reduce-scatter.16.cloned.1.call-done = f32[96,768]{1,0:T(8,128)} async-done(((f32[3072,768]{1,0:T(8,128)}), f32[96,768]{1,0:T(8,128)}) %reduce-scatter.16.cloned.1.call-update) | async-done | bytes 294928 | tf_op jit(solution)/shard_map/reduce_scatter | solution.py:282
  1168.1 41.6 %all-reduce.3 = (f32[12,128]{1,0:T(8,128)S(1)}, f32[768]{0:T(1024)S(1)}, f32[768]{0:T(1024)}, f32[768]{0:T(1024)}, f32[768]{0:T(1024)}, /*index=5*/f32[768]{0:T(1024)}, f32[768]{0:T(1024)}, f32[768]{0:T(1024)}) all-reduce(f32[12,128]{1,0:T(8,128)S(1)} %convolution_bitcast_fusion.6, ...), channel_id=1, replica_groups=mesh['dp'=8,'mp'=4] {'dp','mp'}, use_global_device_ids=true, to_apply=%region_23.24 | all-reduce | flops 6912 | bytes 55296 | tf_op jit(solution)/shard_map/psum | solution.py:301
  1214.5 4.3 convolution_bitcast_fusion.1
  1218.8 3.6 copy.133
  1230.4 52.4 %all-reduce.8.cloned.1.call-done = (f32[768,3,192]{0,2,1:T(8,128)}, f32[192,768]{1,0:T(8,128)}, f32[768,768]{1,0:T(8,128)}, f32[768,768]{1,0:T(8,128)}) async-done(((f32[768,3,192]{0,2,1:T(8,128)}, f32[192,768]{1,0:T(8,128)}, f32[768,768]{1,0:T(8,128)}, f32[768,768]{1,0:T(8,128)}), (f32[768,3,192]{0,2,1:T(8,128)}, f32[192,768]{1,0:T(8,128)}, f32[768,768]{1,0:T(8,128)}, ...) | async-done | bytes 7077904 | tf_op jit(solution)/shard_map/psum | solution.py:318
  (305 shorter events, 106.8 us)
Async XLA Ops:
  7.2 9.4 copy-start
  7.2 76.9 %all-gather.5.cloned.1.call-start = ((), (), s32[]{:S(2)}) async-start(), calls=%async_computation.5 | async-start | bytes 4866048 | tf_op jit(solution)/shard_map/all_gather | solution.py:122
  8.0 9.7 copy-start.67
  8.2 9.6 copy-start.68
  8.2 9.6 copy-start.59
  8.2 10.4 copy-start.20
  17.7 344.8 %reduce-scatter.8.cloned.1.call-start = ((), (), s32[]{:S(2)}) async-start(), calls=%async_computation.6 | async-start | bytes 5898240 | tf_op jit(solution)/shard_map/reduce_scatter | solution.py:177
  17.8 74.6 %copy-start.46 = (f32[768]{0:T(1024)}, f32[768]{0:T(1024)S(1)}, u32[]{:S(2)}) copy-start(f32[768]{0:T(1024)S(1)} %convert_element_type.175) | copy-start | bytes 9220
  93.4 32.0 %copy-start.48 = (f32[768]{0:T(1024)}, f32[768]{0:T(1024)S(1)}, u32[]{:S(2)}) copy-start(f32[768]{0:T(1024)S(1)} %add_rsqrt_fusion.1) | copy-start | bytes 9220
  93.4 33.6 %copy-start.64 = (bf16[2,192]{1,0:T(2,128)(2,1)S(1)}, bf16[2,192]{1,0:T(2,128)(2,1)}, u32[]{:S(2)}) copy-start(bf16[2,192]{1,0:T(2,128)(2,1)} %param.36) | copy-start | bytes 2308
  93.5 33.7 %copy-start.78 = (s32[48]{0:T(128)S(1)}, s32[48]{0:T(128)}, u32[]{:S(2)}) copy-start(s32[48]{0:T(128)} %param.25) | copy-start | bytes 580
  93.8 28.3 %collective-permute-start = (bf16[768,768]{0,1:T(8,128)(2,1)S(1)}, bf16[768,768]{0,1:T(8,128)(2,1)}, u32[]{:S(2)}, u32[]{:S(2)}) collective-permute-start(bf16[768,768]{0,1:T(8,128)(2,1)S(1)} %add_convert_fusion.3), channel_id=1, source_target_pairs={{0,1},{1,0},{2,3},{3,2},{4,5},{5,4},{6,7},{7,6},{8,9},{9,8},{10,11... | collective-permute-start | bytes 3538952 | tf_op jit(solution)/shard_map/ppermute | solution.py:139
  125.4 104.3 %collective-permute-start.1 = (bf16[1536,768]{0,1:T(8,128)(2,1)}, bf16[1536,768]{0,1:T(8,128)(2,1)}, u32[]{:S(2)}, u32[]{:S(2)}) collective-permute-start(bf16[1536,768]{0,1:T(8,128)(2,1)} %maximum_select_fusion.1), channel_id=1, source_target_pairs={{0,2},{1,3},{2,0},{3,1},{4,6},{5,7},{6,4},{7,5},{8,10},{9,11},{10,... | collective-permute-start | bytes 7077896 | tf_op jit(solution)/shard_map/ppermute | solution.py:139
  268.8 6.3 copy-start.17
  278.8 179.0 %all-gather.7.cloned.1.call-start = ((), (), s32[]{:S(2)}) async-start(), calls=%async_computation.7 | async-start | bytes 5898240 | tf_op jit(solution)/shard_map/all_gather | solution.py:188
  367.7 179.9 %all-gather.9.cloned.1.call-start = ((), (), s32[]{:S(2)}) async-start(), calls=%async_computation.9 | async-start | bytes 5898240 | tf_op jit(solution)/shard_map/all_gather | solution.py:201
  370.8 296.8 %reduce-scatter.12.cloned.1.call-start = ((), (), s32[]{:S(2)}) async-start(), calls=%async_computation.10 | async-start | bytes 5898240 | tf_op jit(solution)/shard_map/reduce_scatter | solution.py:210
  547.6 30.6 %copy-start.79 = (bf16[768,768]{1,0:T(8,128)(2,1)S(1)}, bf16[768,768]{1,0:T(8,128)(2,1)}, u32[]{:S(2)}) copy-start(bf16[768,768]{1,0:T(8,128)(2,1)} %param.41) | copy-start | bytes 3538948
  583.8 172.4 %reduce-scatter.10.cloned.1.call-start = ((), (), s32[]{:S(2)}) async-start(), calls=%async_computation.8 | async-start | bytes 5898240 | tf_op jit(solution)/shard_map/reduce_scatter | solution.py:191
  603.8 249.3 %all-gather.11.cloned.1.call-start = ((), (), s32[]{:S(2)}) async-start(), calls=%async_computation.11 | async-start | bytes 5898240 | tf_op jit(solution)/shard_map/all_gather | solution.py:224
  763.0 240.7 %reduce-scatter.14.cloned.1.call-start = ((), (), s32[]{:S(2)}) async-start(), calls=%async_computation.12 | async-start | bytes 5898240 | tf_op jit(solution)/shard_map/reduce_scatter | solution.py:266
  859.5 10.4 slice-start
  864.3 5.5 slice-start.1
  864.3 5.7 copy-start.6
  864.3 6.6 copy-start.10
  919.8 83.9 %copy-start.43 = (f32[768]{0:T(1024)S(1)}, f32[768]{0:T(1024)}, u32[]{:S(2)}) copy-start(f32[768]{0:T(1024)} %copy-done.42) | copy-start | bytes 9220
  919.8 83.9 %copy-start.47 = (f32[768]{0:T(1024)S(1)}, f32[768]{0:T(1024)}, u32[]{:S(2)}) copy-start(f32[768]{0:T(1024)} %copy-done.46) | copy-start | bytes 9220
  919.8 83.9 %copy-start.49 = (f32[768]{0:T(1024)S(1)}, f32[768]{0:T(1024)}, u32[]{:S(2)}) copy-start(f32[768]{0:T(1024)} %copy-done.48) | copy-start | bytes 9220
  919.8 246.0 %reduce-scatter.16.cloned.1.call-start = ((), (), s32[]{:S(2)}) async-start(), calls=%async_computation.13 | async-start | bytes 9732096 | tf_op jit(solution)/shard_map/reduce_scatter | solution.py:282
  1029.0 253.9 %all-reduce.8.cloned.1.call-start = ((), (), s32[]{:S(2)}) async-start(), calls=%async_computation.14 | async-start | bytes 14155776 | tf_op jit(solution)/shard_map/psum | solution.py:318
  1038.6 26.9 %copy-start.12 = (bf16[3072,192]{0,1:T(8,128)(2,1)S(1)}, bf16[3072,192]{0,1:T(8,128)(2,1)}, u32[]{:S(2)}) copy-start(bf16[3072,192]{0,1:T(8,128)(2,1)} %copy-done.11) | copy-start | bytes 3538948
  1080.2 129.6 %copy-start.21 = (bf16[128,768]{1,0:T(8,128)(2,1)S(1)}, bf16[128,768]{1,0:T(8,128)(2,1)}, u32[]{:S(2)}) copy-start(bf16[128,768]{1,0:T(8,128)(2,1)} %param.32) | copy-start | bytes 589828
  1080.2 129.8 %copy-start.25 = (f32[12,128]{1,0:T(8,128)S(1)}, f32[12,128]{1,0:T(8,128)}, u32[]{:S(2)}) copy-start(f32[12,128]{1,0:T(8,128)} %copy-done.24) | copy-start | bytes 18436
  1080.2 129.9 %copy-start.54 = (f32[12]{0:T(128)S(1)}, f32[12]{0:T(128)}, u32[]{:S(2)}) copy-start(f32[12]{0:T(128)} %copy-done.53) | copy-start | bytes 148
  1080.2 130.1 %copy-start.77 = (f32[12]{0:T(128)S(1)}, f32[12]{0:T(128)}, u32[]{:S(2)}) copy-start(f32[12]{0:T(128)} %copy-done.76) | copy-start | bytes 148
  1080.2 130.1 %copy-start.58 = (f32[12]{0:T(128)S(1)}, f32[12]{0:T(128)}, u32[]{:S(2)}) copy-start(f32[12]{0:T(128)} %copy-done.57) | copy-start | bytes 148
  1080.2 130.3 %copy-start.37 = (f32[12,2048]{1,0:T(8,128)S(1)}, f32[12,2048]{1,0:T(8,128)}, u32[]{:S(2)}) copy-start(f32[12,2048]{1,0:T(8,128)} %copy-done.36) | copy-start | bytes 294916
  1089.8 122.4 %copy-start.16 = (bf16[128,2048]{1,0:T(8,128)(2,1)S(1)}, bf16[128,2048]{1,0:T(8,128)(2,1)}, u32[]{:S(2)}) copy-start(bf16[128,2048]{1,0:T(8,128)(2,1)} %param.29) | copy-start | bytes 1572868
  1089.8 122.4 %copy-start.27 = (f32[12,128]{1,0:T(8,128)S(1)}, f32[12,128]{1,0:T(8,128)}, u32[]{:S(2)}) copy-start(f32[12,128]{1,0:T(8,128)} %copy-done.26) | copy-start | bytes 18436
  1089.8 122.4 %copy-start.56 = (f32[12]{0:T(128)S(1)}, f32[12]{0:T(128)}, u32[]{:S(2)}) copy-start(f32[12]{0:T(128)} %copy-done.55) | copy-start | bytes 148
  1089.8 123.1 %copy-start.75 = (f32[12]{0:T(128)S(1)}, f32[12]{0:T(128)}, u32[]{:S(2)}) copy-start(f32[12]{0:T(128)} %copy-done.74) | copy-start | bytes 148
  1089.9 123.1 %copy-start.63 = (f32[12]{0:T(128)S(1)}, f32[12]{0:T(128)}, u32[]{:S(2)}) copy-start(f32[12]{0:T(128)} %copy-done.62) | copy-start | bytes 148
  1089.9 123.3 %copy-start.50 = (bf16[128,128]{1,0:T(8,128)(2,1)S(1)}, bf16[128,128]{1,0:T(8,128)(2,1)}, u32[]{:S(2)}) copy-start(bf16[128,128]{1,0:T(8,128)(2,1)} %param.28) | copy-start | bytes 98308
  1089.9 123.6 %copy-start.29 = (f32[4,12,12]{1,2,0:T(8,128)S(1)}, f32[4,12,12]{1,2,0:T(8,128)}, u32[]{:S(2)}) copy-start(f32[4,12,12]{1,2,0:T(8,128)} %copy-done.28) | copy-start | bytes 6916
  1089.9 123.6 %copy-start.35 = (f32[12,1,4,32]{3,2,1,0:T(4,128)S(1)}, f32[12,1,4,32]{3,2,1,0:T(4,128)}, u32[]{:S(2)}) copy-start(f32[12,1,4,32]{3,2,1,0:T(4,128)} %copy-done.34) | copy-start | bytes 18436
  1089.9 123.6 %copy-start.52 = (f32[4,12]{1,0:T(4,128)S(1)}, f32[4,12]{1,0:T(4,128)}, u32[]{:S(2)}) copy-start(f32[4,12]{1,0:T(4,128)} %copy-done.51) | copy-start | bytes 580
  1166.8 47.1 %copy-start.33 = (f32[12,1,4,32]{3,2,1,0:T(4,128)S(1)}, f32[12,1,4,32]{3,2,1,0:T(4,128)}, u32[]{:S(2)}) copy-start(f32[12,1,4,32]{3,2,1,0:T(4,128)} %copy-done.32) | copy-start | bytes 18436
  1166.8 47.3 %copy-start.31 = (f32[12,1,4,32]{3,2,1,0:T(4,128)S(1)}, f32[12,1,4,32]{3,2,1,0:T(4,128)}, u32[]{:S(2)}) copy-start(f32[12,1,4,32]{3,2,1,0:T(4,128)} %copy-done.30) | copy-start | bytes 18436
  (48 other events, 110.8 us)
Sparse Core Ops, SparseCore 0:
  17.8 66.2 all-gather.4
  278.9 83.5 reduce-scatter.7
  367.8 89.9 all-gather.6
  459.8 87.7 all-gather.8
  583.9 83.6 reduce-scatter.11
  670.4 85.7 reduce-scatter.9
  763.2 89.8 all-gather.10
  920.0 83.6 reduce-scatter.13
  1029.1 136.6 reduce-scatter.15
  1170.5 112.2 all-reduce.7
